TPU v7x, 32 devices: a whole 2x2x4 slice. The times are simulated.
32 devices in a mesh: dp: 16 (over z, y, x), tensor: 2 (over core).
Axes of the slice: x: 2, y: 2, z: 4, core: 2. Of those that a mesh axis runs over, the one named last changes fastest.
Arguments:
- gradient: bfloat16 [16, 128, 8192], P('dp', 'tensor'), may hold values from -110 to 110
- momentum: bfloat16 [16, 128, 8192], P('dp', 'tensor'), may hold values from -6 to 6
- indices: int32 [16, 2, 128, 32], P('dp', 'tensor'), may hold values from 0 to 4095, all different within a row
Outputs:
- new_momentum: bfloat16 [16, 128, 8192], P('dp', 'tensor')
- update: bfloat16 [128, 8192], P('tensor')
Inputs may be any that keep to these rules, and one draw needn't show every extreme that they name: The 32 indices of one span of one replica are distinct; index a * 64 + b names row frequency a and column frequency b.
All inputs are finite; a program needn't handle non-finite values.
Results may differ from a plain program's by a relative error of at most 0.0049.
Values may be sent and summed in bfloat16 or wider, within the bound.
A program may use at most 64 MiB of HBM per device.

v0:
```python
import jax
import jax.numpy as jnp
from jax import lax
from jax.sharding import PartitionSpec as P

BLOCK = 64


EPSILON = 1e-06
DECAY = 0.999


def dct_basis(block_edge):
    frequency = jnp.arange(block_edge, dtype=jnp.float32)[:, None]
    position = jnp.arange(block_edge, dtype=jnp.float32)[None, :]
    waves = jnp.cos(jnp.pi * (2.0 * position + 1.0) * frequency / (2.0 * block_edge))
    weights = jnp.where(frequency == 0.0, jnp.sqrt(1.0 / block_edge), jnp.sqrt(2.0 / block_edge))
    return waves * weights


def to_spans(slab, block_edge):
    height, columns = slab.shape
    shaped = slab.reshape(height // block_edge, block_edge, columns // block_edge, block_edge)
    return shaped.transpose(0, 2, 1, 3).reshape(-1, block_edge, block_edge)


def from_spans(blocks, height, columns):
    block_edge = blocks.shape[-1]
    shaped = blocks.reshape(height // block_edge, columns // block_edge, block_edge, block_edge)
    return shaped.transpose(0, 2, 1, 3).reshape(height, columns)


def inverse(spectra, cosines):
    return jnp.einsum("ka,ckl,lb->cab", cosines, spectra, cosines, precision=lax.Precision.HIGHEST)


def densify(shipped, chosen, block_edge):
    sources, number, selected = shipped.shape
    merged_values = shipped.transpose(1, 0, 2).reshape(number, sources * selected)
    merged_ids = chosen.transpose(1, 0, 2).reshape(number, sources * selected)
    levels = jnp.arange(block_edge, dtype=jnp.int32)[None, :, None]
    row_hits = jnp.where(
        (merged_ids // block_edge)[:, None, :] == levels,
        merged_values[:, None, :],
        jnp.zeros((), jnp.bfloat16),
    )
    col_hits = ((merged_ids % block_edge)[:, None, :] == levels).astype(jnp.bfloat16)
    return jnp.einsum("caj,cbj->cab", row_hits, col_hits, preferred_element_type=jnp.float32)


def local(gradient, momentum, indices):
    block_edge = BLOCK
    cosines = dct_basis(block_edge)
    precise = lax.Precision.HIGHEST
    height = gradient.shape[1]
    columns = gradient.shape[2]
    renewed = DECAY * momentum[0].astype(jnp.float32) + gradient[0].astype(jnp.float32)
    spectra = jnp.einsum(
        "ka,cab,lb->ckl", cosines, to_spans(renewed, block_edge), cosines, precision=precise
    )
    span_count = spectra.shape[0]
    chosen = indices[0].reshape(span_count, indices.shape[-1])
    levels = jnp.arange(block_edge, dtype=jnp.int32)[None, None, :]
    row_pick = ((chosen // block_edge)[:, :, None] == levels).astype(jnp.float32)
    col_pick = ((chosen % block_edge)[:, :, None] == levels).astype(jnp.float32)
    partial_value = jnp.einsum("cka,cab->ckb", row_pick, spectra, precision=precise)
    picked = jnp.sum(partial_value * col_pick, axis=2)
    marker = jnp.einsum("cka,ckb->cab", row_pick, col_pick, precision=precise)
    restored = inverse(spectra * marker, cosines)
    new_momentum = (renewed - from_spans(restored, height, columns)).astype(jnp.bfloat16)[None]
    values = picked.astype(jnp.bfloat16)
    element_total = height * columns * lax.axis_size("tensor")
    replicas = lax.axis_size("dp")
    owned_count = span_count // replicas
    outgoing = (
        values.reshape(replicas, owned_count, -1),
        chosen.reshape(replicas, owned_count, -1),
    )
    owned = inverse(
        densify(
            lax.all_to_all(outgoing[0], "dp", split_axis=0, concat_axis=0, tiled=True),
            lax.all_to_all(outgoing[1], "dp", split_axis=0, concat_axis=0, tiled=True),
            block_edge,
        ),
        cosines,
    )
    energy = lax.psum(jnp.sum(owned * owned), ("dp", "tensor"))
    scaled = (owned / jnp.sqrt(energy / element_total + EPSILON)).astype(jnp.bfloat16)
    whole = lax.all_gather(scaled, "dp", axis=0, tiled=True)
    update = from_spans(whole, height, columns)
    return (new_momentum, update)


def solution(mesh):
    in_specs = (P("dp", "tensor", None), P("dp", "tensor", None), P("dp", "tensor", None, None))
    out_specs = (P("dp", "tensor", None), P("tensor", None))
    return jax.shard_map(local, mesh=mesh, in_specs=in_specs, out_specs=out_specs, check_vma=False)
```

profile of v0, /device:TPU:0, one launch (start us, length us, event | category | flops | bytes accessed | tf_op | source)
XLA Modules:
  0.0 186.2 jit_solution(10111530458172465902)
XLA Ops:
  7.2 1.8 convert_add_fusion
  9.0 3.0 %add.71 = f32[1,64,128,64]{3,2,1,0:T(8,128)} reshape(f32[1,64,8192]{2,1,0:T(8,128)S(1)} %convert_add_fusion) | data formatting | bytes 4194304 | tf_op jit(solution)/shard_map/add | solution.py:57
  12.0 0.0 copy-start.2
  12.0 3.5 %copy.34 = f32[128,64,64]{0,1,2:T(8,128)S(1)} copy(f32[128,64,64]{2,0,1:T(8,128)} %bitcast.69) | data formatting | bytes 4194304 | tf_op jit(solution)/shard_map/reshape | solution.py:24
  15.6 0.0 copy-done.2
  15.6 0.1 copy.36
  15.7 0.1 copy.37
  15.8 4.3 %fusion.6 = f32[128,64,64]{2,1,0:T(8,128)} fusion(s32[128,32]{1,0:T(8,128)S(1)} %copy.37, s32[128,32]{1,0:T(8,128)S(1)} %copy.36), kind=kOutput, calls=%fused_computation.9 | convolution fusion | flops 34078720 | bytes 2129920 | tf_op jit(solution)/shard_map/cka,ckb->cab/dot_general | solution.py:68
  20.1 4.8 %copy.38 = f32[128,64,64]{0,2,1:T(8,128)} copy(f32[128,64,64]{2,1,0:T(8,128)} %fusion.6) | data formatting | bytes 4194304 | tf_op jit(solution)/shard_map/cka,ckb->cab/dot_general | solution.py:68
  24.9 0.0 copy-start
  24.9 2.2 %fusion.28 = f32[128,64,64]{0,2,1:T(8,128)S(1)} fusion(f32[128,64,64]{0,1,2:T(8,128)S(1)} %copy.34, f32[64]{0:T(128)S(1)} %get-tuple-element.10, f32[64]{0:T(128)S(1)} %get-tuple-element.11), kind=kOutput, calls=%fused_computation.34 | convolution fusion | flops 402665472 | bytes 4194816 | tf_op jit(solution)/shard_map/ka,cab,lb->ckl/dot_general | solution.py:58
  27.1 0.0 copy-done
  27.1 4.7 %fusion.60 = (f32[128,64,64]{0,2,1:T(8,128)S(1)}, f32[128,64,64]{0,2,1:T(8,128)}) fusion(f32[128,64,64]{0,2,1:T(8,128)S(1)} %copy-done, f32[64]{0:T(128)S(1)} %get-tuple-element.10, f32[64]{0:T(128)S(1)} %get-tuple-element.11, f32[128,64,64]{0,2,1:T(8,128)S(1)} %fusion.28), kind=kOutput, calls=%fused_computation.83 | convolution fusion | flops 403189760 | bytes 8389120 | tf_op jit(solution)/shard_map/ka,cab,lb->ckl/dot_general | solution.py:58
  31.8 5.6 %copy.46 = f32[128,64,64]{2,1,0:T(8,128)} copy(f32[128,64,64]{0,2,1:T(8,128)} %get-tuple-element.7) | data formatting | bytes 4194304 | tf_op jit(solution)/shard_map/ka,cab,lb->ckl/dot_general | solution.py:58
  37.4 5.2 %select_reduce_fusion = bf16[128,32]{1,0:T(8,128)(2,1)S(1)} fusion(f32[128,64,64]{2,1,0:T(8,128)} %copy.46, s32[128,32]{1,0:T(8,128)S(1)} %copy.37, s32[128,32]{1,0:T(8,128)S(1)} %copy.36), kind=kOutput, calls=%fused_computation.6 | convolution fusion | flops 202371072 | bytes 2138112 | tf_op jit(solution)/shard_map/cka,cab->ckb/dot_general | solution.py:66
  42.5 0.7 reshape.184
  43.2 8.3 %all-to-all-start.1 = ((bf16[16,2,128]{2,1,0:T(2,128)(2,1)}), bf16[16,2,128]{2,1,0:T(2,128)(2,1)S(1)}, u32[]{:S(2)}, u32[]{:S(2)}) async-start(bf16[16,2,128]{2,1,0:T(2,128)(2,1)} %reshape.184), calls=%async_computation.1 | async-start | bytes 16384 | tf_op jit(solution)/shard_map/all_to_all | solution.py:81
  51.6 0.1 copy.44
  51.7 0.7 reshape.182
  52.4 6.4 %all-to-all-done.1 = bf16[16,2,128]{2,1,0:T(2,128)(2,1)S(1)} async-done(((bf16[16,2,128]{2,1,0:T(2,128)(2,1)}), bf16[16,2,128]{2,1,0:T(2,128)(2,1)S(1)}, u32[]{:S(2)}, u32[]{:S(2)}) %all-to-all-start.1) | async-done | bytes 8224 | tf_op jit(solution)/shard_map/all_to_all | solution.py:81
  58.8 3.5 %all-to-all-start = ((s32[16,1,256]{2,1,0:T(1,128)}), s32[16,1,256]{2,1,0:T(1,128)S(1)}, u32[]{:S(2)}, u32[]{:S(2)}) async-start(s32[16,1,256]{2,1,0:T(1,128)} %reshape.182), calls=%async_computation | async-start | bytes 32768 | tf_op jit(solution)/shard_map/all_to_all | solution.py:82
  62.3 0.0 all-gather.2.cloned.1.call-start
  62.4 4.7 %fusion.2 = f32[128,64,64]{0,2,1:T(8,128)} fusion(f32[128,64,64]{0,2,1:T(8,128)S(1)} %get-tuple-element.6, f32[64]{0:T(128)S(1)} %get-tuple-element.10, f32[64]{0:T(128)S(1)} %get-tuple-element.11), kind=kOutput, calls=%fused_computation.2 | convolution fusion | flops 402665472 | bytes 4194816 | tf_op jit(solution)/shard_map/ka,ckl,lb->cab/dot_general | solution.py:34
  67.1 0.1 reshape.185
  67.2 0.1 broadcast_in_dim.33
  67.3 2.3 %all-to-all-done = s32[16,1,256]{2,1,0:T(1,128)S(1)} async-done(((s32[16,1,256]{2,1,0:T(1,128)}), s32[16,1,256]{2,1,0:T(1,128)S(1)}, u32[]{:S(2)}, u32[]{:S(2)}) %all-to-all-start) | async-done | bytes 16416 | tf_op jit(solution)/shard_map/all_to_all | solution.py:82
  69.6 0.5 broadcast.162
  70.1 0.7 reduce
  70.8 0.1 reshape.183
  70.9 0.1 reshape.176
  71.1 0.3 fusion.15
  71.4 1.0 fusion.25
  72.4 1.1 multiply_reduce_fusion
  73.5 38.4 %psum.7 = f32[]{:T(128)} all-reduce(f32[]{:T(128)} %get-tuple-element.8), channel_id=1, replica_groups=mesh['dp'=16,'tensor'=2] {'dp','tensor'}, use_global_device_ids=true, to_apply=%region_2.3 | all-reduce | flops 1 | bytes 8 | tf_op jit(solution)/shard_map/psum | solution.py:87
  112.6 0.7 divide_convert_fusion
  113.3 0.0 all-gather.2.cloned.1.call-update
  113.3 4.9 %fusion.8 = f32[1,64,128,64]{2,3,1,0:T(8,128)S(1)} fusion(f32[128,64,64]{0,2,1:T(8,128)} %fusion.2, f32[64]{0:T(128)S(1)} %get-tuple-element.10, f32[64]{0:T(128)S(1)} %get-tuple-element.11), kind=kOutput, calls=%fused_computation.13 | convolution fusion | flops 402665472 | bytes 4194816 | tf_op jit(solution)/shard_map/ka,ckl,lb->cab/dot_general | solution.py:34
  118.2 2.7 %copy.43 = f32[1,64,128,64]{3,2,1,0:T(8,128)} copy(f32[1,64,128,64]{2,3,1,0:T(8,128)S(1)} %fusion.8) | data formatting | bytes 4194304 | tf_op jit(solution)/shard_map/transpose | solution.py:30
  120.9 0.0 copy-start.1
  120.9 3.6 %reshape.175 = f32[1,64,8192]{2,1,0:T(8,128)S(1)} reshape(f32[1,64,128,64]{3,2,1,0:T(8,128)} %copy.43) | data formatting | bytes 4194304 | tf_op jit(solution)/shard_map/reshape | solution.py:30
  124.6 0.0 copy-done.1
  124.6 2.6 %subtract_convert_fusion = bf16[1,64,8192]{2,1,0:T(8,128)(2,1)} fusion(f32[1,64,8192]{2,1,0:T(8,128)S(1)} %reshape.175, bf16[1,64,8192]{2,1,0:T(8,128)(2,1)S(1)} %copy-done.1, bf16[1,64,8192]{2,1,0:T(8,128)(2,1)} %param.4), kind=kLoop, calls=%fused_computation.7 | loop fusion | flops 3145728 | bytes 5242880 | tf_op jit(solution)/shard_map/convert_element_type | solution.py:70
  127.1 46.8 %all-gather.2.cloned.1.call-done = bf16[128,64,64]{2,1,0:T(8,128)(2,1)} async-done(((bf16[8,64,64]{2,1,0:T(8,128)(2,1)}), bf16[128,64,64]{2,1,0:T(8,128)(2,1)}) %all-gather.2.cloned.1.call-update) | async-done | bytes 1048592 | tf_op jit(solution)/shard_map/all_gather | solution.py:89
  173.9 2.9 %copy.50 = bf16[1,64,128,64]{3,2,1,0:T(8,128)(2,1)S(1)} copy(bf16[1,64,128,64]{3,1,2,0:T(8,128)(2,1)} %bitcast.70) | data formatting | bytes 2097152 | tf_op jit(solution)/shard_map/transpose | solution.py:30
  176.9 2.5 %reshape.178 = bf16[64,8192]{1,0:T(8,128)(2,1)} reshape(bf16[1,64,128,64]{3,2,1,0:T(8,128)(2,1)S(1)} %copy.50) | data formatting | bytes 2097152 | tf_op jit(solution)/shard_map/reshape | solution.py:30
  (5 shorter events, 0.1 us)
Async XLA Ops:
  12.0 3.5 %copy-start.2 = (s32[1,1,128,32]{2,3,1,0:T(8,128)S(1)}, s32[1,1,128,32]{2,3,1,0:T(8,128)}, u32[]{:S(2)}) copy-start(s32[1,1,128,32]{2,3,1,0:T(8,128)} %param.5) | copy-start | bytes 49156
  24.9 2.2 %copy-start = (f32[128,64,64]{0,2,1:T(8,128)S(1)}, f32[128,64,64]{0,2,1:T(8,128)}, u32[]{:S(2)}) copy-start(f32[128,64,64]{0,2,1:T(8,128)} %copy.38) | copy-start | bytes 6291460
  43.2 15.6 %all-to-all-start.1 = ((bf16[16,2,128]{2,1,0:T(2,128)(2,1)}), bf16[16,2,128]{2,1,0:T(2,128)(2,1)S(1)}, u32[]{:S(2)}, u32[]{:S(2)}) async-start(bf16[16,2,128]{2,1,0:T(2,128)(2,1)} %reshape.184), calls=%async_computation.1 | async-start | bytes 16384 | tf_op jit(solution)/shard_map/all_to_all | solution.py:81
  58.8 10.8 %all-to-all-start = ((s32[16,1,256]{2,1,0:T(1,128)}), s32[16,1,256]{2,1,0:T(1,128)S(1)}, u32[]{:S(2)}, u32[]{:S(2)}) async-start(s32[16,1,256]{2,1,0:T(1,128)} %reshape.182), calls=%async_computation | async-start | bytes 32768 | tf_op jit(solution)/shard_map/all_to_all | solution.py:82
  62.3 111.6 %all-gather.2.cloned.1.call-start = ((), (), s32[]{:S(2)}) async-start(), calls=%async_computation.2 | async-start | bytes 2228224 | tf_op jit(solution)/shard_map/all_gather | solution.py:89
  120.9 3.7 %copy-start.1 = (bf16[1,64,8192]{2,1,0:T(8,128)(2,1)S(1)}, bf16[1,64,8192]{2,1,0:T(8,128)(2,1)}, u32[]{:S(2)}) copy-start(bf16[1,64,8192]{2,1,0:T(8,128)(2,1)} %param.3) | copy-start | bytes 3145732
Sparse Core Ops, SparseCore 0:
  113.4 60.4 all-gather.1
where the time goes:
time: 187 us; the launch traced here: 186 us
  waiting for transfers between devices  55.5 us (30%)
  blocking collectives  38.4 us (21%)
  local copies, waits for them, and re-layouts  31.3 us (17%)
  matrix products  28.4 us (15%)
  between operations  14.9 us (8%)
  starting transfers between devices  11.9 us (6%)
  other arithmetic  5.81 us (3%)
    all_gather x1, waiting for transfers between devices, local(): whole = lax.all_gather(scaled, 'dp', axis=0, tiled=True)  46.8 us
    psum x1, blocking collectives, local(): energy = lax.psum(jnp.sum(owned * owned), ('dp', 'tensor'))  38.4 us
    dot_general x4, matrix products, inverse(): jnp.einsum('ka,ckl,lb->cab', cosines, spectra, cosines, precision=lax.Pre...  11.7 us
    all_to_all x1, starting transfers between devices, local(): lax.all_to_all(outgoing[0], 'dp', split_axis=0, concat_axis=0, tiled=True)  8.35 us
    dot_general x2, matrix products, local(): jnp.einsum('ka,cab,lb->ckl', cosines, to_spans(renewed, block_edge), cosi...  6.88 us
    all_to_all x1, waiting for transfers between devices, local(): lax.all_to_all(outgoing[0], 'dp', split_axis=0, concat_axis=0, tiled=True)  6.42 us
    reshape x2, local copies, waits for them, and re-layouts, from_spans(): return shaped.transpose(0, 2, 1, 3).reshape(height, columns)  6.13 us
    transpose x2, local copies, waits for them, and re-layouts, from_spans(): return shaped.transpose(0, 2, 1, 3).reshape(height, columns)  5.67 us
  transfers between devices with their start and end apart: 3, of which 3 were waited for; matrix products, arithmetic and copies ran while one was open for 10% of the time, Pallas kernels for 0%

commit v1 on v0

v1 whole, which is shorter than its diff:
```python
import functools

import jax
import jax.numpy as jnp
import numpy as np
from jax import lax
from jax.experimental import pallas as pl
from jax.experimental.pallas import tpu as pltpu
from jax.sharding import PartitionSpec as P

BLOCK = 64
LANES = 128
EPSILON = 1e-06
DECAY = 0.999
F32 = jnp.float32
BF16 = jnp.bfloat16
MESH = pl.DeviceIdType.MESH


def dct_basis(edge):
    frequency = np.arange(edge, dtype=np.float64)[:, None]
    position = np.arange(edge, dtype=np.float64)[None, :]
    waves = np.cos(np.pi * (2.0 * position + 1.0) * frequency / (2.0 * edge))
    weights = np.where(frequency == 0.0, np.sqrt(1.0 / edge), np.sqrt(2.0 / edge))
    return (waves * weights).astype(np.float32)


def halves(x):
    high = x.astype(BF16)
    return high, (x - high.astype(F32)).astype(BF16)


def np_halves(x):
    high = x.astype(jnp.bfloat16)
    return high, (x - high.astype(np.float32)).astype(jnp.bfloat16)


def dot(a, b):
    return jnp.dot(a, b, preferred_element_type=F32)


def dot_nt(a, b):
    return lax.dot_general(a, b, (((1,), (1,)), ((), ())), preferred_element_type=F32)


def wide(x, w_high, w_low):
    rows = x.shape[0]
    high, low = halves(x)
    both = dot(jnp.concatenate([high, low], axis=0), w_high)
    return both[:rows] + both[rows:] + dot(high, w_low)


def kernel(
    replicas, shards, unroll, total,
    grad_ref, mom_ref, idx_ref, fwd_ref, inv_ref, rows_ref, rows3_ref,
    newm_ref, upd_ref,
    payload, landed, span_a, span_b, span_v, picks, values, dense, e_out, e_in,
    send_sem, recv_sem, e_send, e_recv,
):
    me = lax.axis_index("dp")
    part = lax.axis_index("tensor")
    barrier = pltpu.get_barrier_semaphore()

    def greet_dp(k, c):
        pl.semaphore_signal(barrier, inc=1, device_id={"dp": lax.rem(me + k, replicas)}, device_id_type=MESH)
        return c

    def greet_tp(k, c):
        pl.semaphore_signal(barrier, inc=1, device_id={"tensor": lax.rem(part + k, shards)}, device_id_type=MESH)
        return c

    lax.fori_loop(1, replicas, greet_dp, 0)
    lax.fori_loop(1, shards, greet_tp, 0)

    topk = idx_ref.shape[1]
    fold = LANES // topk
    width = fold * BLOCK
    groups = grad_ref.shape[1] // width

    chosen = jnp.concatenate(
        [idx_ref[pl.ds(s, groups, stride=fold), :] for s in range(fold)], axis=1
    )
    payload[1] = (chosen // BLOCK).astype(F32).astype(BF16)
    payload[2] = (chosen % BLOCK).astype(F32).astype(BF16)
    picks[0] = chosen // BLOCK
    picks[1] = chosen % BLOCK + BLOCK * (lax.broadcasted_iota(jnp.int32, chosen.shape, 1) // topk)

    tall = lax.broadcasted_iota(jnp.int32, (width, LANES), 0)
    short = lax.broadcasted_iota(jnp.int32, (BLOCK, LANES), 0)

    def masks(g):
        row_hot = (short == picks[0, pl.ds(g, 1), :]).astype(F32).astype(BF16)
        col_hot = (tall == picks[1, pl.ds(g, 1), :]).astype(F32).astype(BF16)
        return row_hot, col_hot

    def columns(g):
        return pl.ds(pl.multiple_of(g * width, width), width)

    def encode(step, c):
        batch = [step * unroll + u for u in range(unroll)]
        for g in batch:
            cols = columns(g)
            renewed = DECAY * mom_ref[:, cols].astype(F32) + grad_ref[:, cols].astype(F32)
            row_hot, col_hot = masks(g)
            part_spec = wide(renewed, fwd_ref[0], fwd_ref[1])
            high, low = halves(part_spec)
            both = dot(jnp.concatenate([high, low], axis=0), col_hot)
            lines = both[:BLOCK] + both[BLOCK:]
            waves = dot(rows_ref[...], jnp.concatenate([row_hot, row_hot], axis=0))
            value = jnp.sum(lines * waves, axis=0, keepdims=True)
            values[pl.ds(g, 1), :] = value
            high, low = halves(waves * value)
            spread = dot_nt(high, col_hot) + dot_nt(low, col_hot)
            restored = wide(spread, inv_ref[0], inv_ref[1])
            newm_ref[:, cols] = (renewed - restored).astype(BF16)
        return c

    lax.fori_loop(0, groups // unroll, encode, 0)
    payload[0] = values[...].astype(BF16)
    pl.semaphore_wait(barrier, replicas - 1 + shards - 1)

    def copy_dp(k, slot):
        return pltpu.make_async_remote_copy(
            src_ref=payload, dst_ref=landed.at[slot],
            send_sem=send_sem.at[k], recv_sem=recv_sem.at[k],
            device_id={"dp": lax.rem(me + k, replicas)}, device_id_type=MESH,
        )

    def start_dp(k, c):
        copy_dp(k, me).start()
        return c

    lax.fori_loop(1, replicas, start_dp, 0)
    landed[me] = payload[...]

    def finish_dp(k, c):
        copy_dp(k, lax.rem(me - k + replicas, replicas)).wait_recv()
        return c

    lax.fori_loop(1, replicas, finish_dp, 0)

    for plane, target in enumerate((span_v, span_a, span_b)):
        for s in range(fold):
            target[s * groups:(s + 1) * groups, :] = jnp.concatenate(
                [landed[r, plane].astype(F32)[:, s * topk:(s + 1) * topk] for r in range(replicas)], axis=1
            )

    depth = replicas * topk
    level = lax.broadcasted_iota(jnp.int32, (BLOCK, depth), 0).astype(F32).astype(BF16)
    zero = jnp.zeros((), BF16)
    one = jnp.ones((), BF16)

    def densify(step, energy):
        tiles = []
        for s in range(fold):
            lines = pl.ds(pl.multiple_of(s * groups + step * 8, 8), 8)
            tiles.append([ref[lines, :] for ref in (span_a, span_b, span_v)])
        for u in range(8):
            blocks = []
            for s in range(fold):
                a, b, v = (tile[u:u + 1].astype(BF16) for tile in tiles[s])
                row_hot = jnp.where(level == a, v, zero)
                col_hot = jnp.where(level == b, one, zero)
                blocks.append(dot_nt(row_hot, col_hot))
            combined = jnp.concatenate(blocks, axis=1)
            dense[:, columns(step * 8 + u)] = combined
            energy = energy + jnp.sum((combined * combined).reshape(BLOCK // 8, 8, width), axis=0)
        return energy

    energy = lax.fori_loop(0, groups // 8, densify, jnp.zeros((8, width), F32))
    energy = sum(energy[:, n * LANES:(n + 1) * LANES] for n in range(width // LANES))
    e_out[...] = energy
    e_in[part] = energy

    def copy_tp(k, slot):
        return pltpu.make_async_remote_copy(
            src_ref=e_out, dst_ref=e_in.at[slot],
            send_sem=e_send.at[k], recv_sem=e_recv.at[k],
            device_id={"tensor": lax.rem(part + k, shards)}, device_id_type=MESH,
        )

    def start_tp(k, c):
        copy_tp(k, part).start()
        return c

    lax.fori_loop(1, shards, start_tp, 0)

    def decode(step, c):
        for u in range(unroll):
            cols = columns(step * unroll + u)
            high, low = halves(wide(dense[:, cols], inv_ref[0], inv_ref[1]))
            dense[:, cols] = dot(rows3_ref[...], jnp.concatenate([high, high, low], axis=0))
        return c

    lax.fori_loop(0, groups // unroll, decode, 0)

    def finish_tp(k, c):
        copy_tp(k, lax.rem(part - k + shards, shards)).wait()
        return c

    lax.fori_loop(1, shards, finish_tp, 0)
    mean = jnp.sum(e_in[...]) / total
    scale = lax.rsqrt(jnp.full((1, width), mean + EPSILON, F32))

    def finish(g, c):
        cols = columns(g)
        upd_ref[:, cols] = (dense[:, cols] * scale).astype(BF16)
        return c

    lax.fori_loop(0, groups, finish, 0)

    def sent_dp(k, c):
        copy_dp(k, me).wait_send()
        return c

    lax.fori_loop(1, replicas, sent_dp, 0)


def local(gradient, momentum, indices, replicas, shards):
    height, cols = gradient.shape[1:]
    topk = indices.shape[-1]
    fold = LANES // topk
    spans = cols // BLOCK
    groups = spans // fold
    assert height == BLOCK and groups * fold == spans
    basis = dct_basis(BLOCK)
    eye = np.eye(fold, dtype=np.float32)
    fwd = jnp.asarray(np.stack(np_halves(np.kron(eye, basis.T))))
    inv = jnp.asarray(np.stack(np_halves(np.kron(eye, basis))))
    high, low = np_halves(basis.T)
    rows = jnp.asarray(np.concatenate([high, low], axis=1))
    rows3 = jnp.asarray(np.concatenate([high, low, high], axis=1))
    depth = max(replicas * topk, LANES)
    vmem = pl.BlockSpec(memory_space=pltpu.VMEM)
    newm, update = pl.pallas_call(
        functools.partial(kernel, replicas, shards, 4, float(height * cols * shards)),
        out_shape=(
            jax.ShapeDtypeStruct((height, cols), BF16),
            jax.ShapeDtypeStruct((height, cols), BF16),
        ),
        in_specs=[vmem] * 7,
        out_specs=(vmem, vmem),
        scratch_shapes=[
            pltpu.VMEM((3, groups, LANES), BF16),
            pltpu.VMEM((replicas, 3, groups, LANES), BF16),
            pltpu.VMEM((spans, depth), F32),
            pltpu.VMEM((spans, depth), F32),
            pltpu.VMEM((spans, depth), F32),
            pltpu.VMEM((2, groups, LANES), jnp.int32),
            pltpu.VMEM((groups, LANES), F32),
            pltpu.VMEM((height, cols), F32),
            pltpu.VMEM((8, LANES), F32),
            pltpu.VMEM((shards, 8, LANES), F32),
            pltpu.SemaphoreType.DMA((replicas,)),
            pltpu.SemaphoreType.DMA((replicas,)),
            pltpu.SemaphoreType.DMA((shards,)),
            pltpu.SemaphoreType.DMA((shards,)),
        ],
        compiler_params=pltpu.CompilerParams(collective_id=0, has_side_effects=True),
        name="demo_step",
    )(gradient[0], momentum[0], indices.reshape(spans, topk), fwd, inv, rows, rows3)
    return newm[None], update


def solution(mesh):
    in_specs = (P("dp", "tensor", None), P("dp", "tensor", None), P("dp", "tensor", None, None))
    out_specs = (P("dp", "tensor", None), P("tensor", None))
    body = functools.partial(local, replicas=mesh.shape["dp"], shards=mesh.shape["tensor"])
    return jax.shard_map(body, mesh=mesh, in_specs=in_specs, out_specs=out_specs, check_vma=False)
```

time: 187 us -> 50.4 us (0.27)
  waiting for transfers between devices: 55.5 us -> 0 us
  Pallas kernels: 0 us -> 44.7 us
  blocking collectives: 38.4 us -> 0 us
  matrix products: 28.4 us -> 0 us
  local copies, waits for them, and re-layouts: 31.3 us -> 4.77 us
  between operations: 14.9 us -> 0.65 us
  starting transfers between devices: 11.9 us -> 0 us
  other arithmetic: 5.81 us -> 0 us
    all_gather x1 -> x0, waiting for transfers between devices: 46.8 us -> none  [local(): whole = lax.all_gather(scaled, 'dp', axis=0, tiled=True)]
    pallas_call x0 -> x1, Pallas kernels: none -> 44.7 us  [local(): pl.pallas_call(functools.partial(kernel, replicas, shards, 4, float(heigh...]
    psum x1 -> x0, blocking collectives: 38.4 us -> none  [local(): energy = lax.psum(jnp.sum(owned * owned), ('dp', 'tensor'))]
    dot_general x9 -> x0, matrix products: 28.4 us -> none  [the longest x4 11.7 us: inverse(): jnp.einsum('ka,ckl,lb->cab', cosines, spectra, cosines, precision=lax.Pre...]
    all_to_all x2 -> x0, starting transfers between devices: 11.8 us -> none  [the longest x1 8.35 us: local(): lax.all_to_all(outgoing[0], 'dp', split_axis=0, concat_axis=0, tiled=True)]
    dot_general x2 -> x0, local copies, waits for them, and re-layouts: 10.4 us -> none  [the longest x1 5.57 us: local(): jnp.einsum('ka,cab,lb->ckl', cosines, to_spans(renewed, block_edge), cosi...]
    reshape x4 -> x0, local copies, waits for them, and re-layouts: 9.76 us -> none  [the longest x2 6.13 us: from_spans(): return shaped.transpose(0, 2, 1, 3).reshape(height, columns)]
    all_to_all x2 -> x0, waiting for transfers between devices: 8.74 us -> none  [the longest x1 6.42 us: local(): lax.all_to_all(outgoing[0], 'dp', split_axis=0, concat_axis=0, tiled=True)]
  transfers between devices with their start and end apart: 3 -> 0, of which waited for: 3 -> 0; matrix products, arithmetic and copies ran while one was open for 10% -> 0% of each run, Pallas kernels for 0% -> 0%
where the time goes in v1:
time: 50.4 us; the launch traced here: 50.1 us
  Pallas kernels  44.7 us (89%)
  local copies, waits for them, and re-layouts  4.77 us (9%)
  between operations  0.65 us (1%)
    pallas_call x1, Pallas kernels, local(): pl.pallas_call(functools.partial(kernel, replicas, shards, 4, float(heigh...  44.7 us
    unnamed x5, local copies, waits for them, and re-layouts  4.77 us

profile of v1, /device:TPU:0, one launch (start us, length us, event | category | flops | bytes accessed | tf_op | source)
XLA Modules:
  0.0 50.1 jit_solution(5832780097214920865)
XLA Ops:
  0.6 1.4 %copy.9 = s32[1,1,128,32]{3,2,1,0:T(8,128)} copy(s32[1,1,128,32]{2,3,1,0:T(8,128)} %param.9) | data formatting | bytes 32768 | tf_op args[2]
  2.1 44.7 %demo_step.1 = (bf16[64,8192]{1,0:T(8,128)(2,1)}, bf16[64,8192]{1,0:T(8,128)(2,1)}) custom-call(bf16[64,8192]{1,0:T(8,128)(2,1)} %bitcast.5, bf16[64,8192]{1,0:T(8,128)(2,1)} %bitcast.6, s32[128,32]{1,0:T(8,128)} %bitcast.7, bf16[2,256,256]{2,1,0:T(8,128)(2,1)} %constant.8.clone.fwd_ref, bf16[2,256,256]{2,1,0:T(8,128)(2,1)} %constant.9.clone.inv_ref, ...), custom_call_target="tpu_custom_call" | custom-call | tf_op jit(solution)/shard_map/demo_step/pallas_call | solution.py:235
  46.8 0.0 copy-start
  46.8 2.4 %copy.12 = bf16[1,64,8192]{2,1,0:T(8,128)(2,1)} copy(bf16[1,64,8192]{2,1,0:T(8,128)(2,1)} %bitcast.4) | data formatting | bytes 2097152
  49.1 0.0 copy-done
  49.1 1.0 %copy.13 = bf16[64,8192]{1,0:T(8,128)(2,1)} copy(bf16[64,8192]{1,0:T(8,128)(2,1)S(1)} %copy-done) | data formatting | bytes 2097152
Async XLA Ops:
  46.8 2.4 %copy-start = (bf16[64,8192]{1,0:T(8,128)(2,1)S(1)}, bf16[64,8192]{1,0:T(8,128)(2,1)}, u32[]{:S(2)}) copy-start(bf16[64,8192]{1,0:T(8,128)(2,1)} %get-tuple-element.9) | copy-start | bytes 3145732

commit v2 on v1

v2 whole, which is shorter than its diff:
```python
import functools

import jax
import jax.numpy as jnp
import numpy as np
from jax import lax
from jax.experimental import pallas as pl
from jax.experimental.pallas import tpu as pltpu
from jax.sharding import PartitionSpec as P

BLOCK = 64
LANES = 128
EPSILON = 1e-06
DECAY = 0.999
F32 = jnp.float32
BF16 = jnp.bfloat16
MESH = pl.DeviceIdType.MESH


def dct_basis(edge):
    frequency = np.arange(edge, dtype=np.float64)[:, None]
    position = np.arange(edge, dtype=np.float64)[None, :]
    waves = np.cos(np.pi * (2.0 * position + 1.0) * frequency / (2.0 * edge))
    weights = np.where(frequency == 0.0, np.sqrt(1.0 / edge), np.sqrt(2.0 / edge))
    return (waves * weights).astype(np.float32)


def halves(x):
    high = x.astype(BF16)
    return high, (x - high.astype(F32)).astype(BF16)


def np_halves(x):
    high = x.astype(jnp.bfloat16)
    return high, (x - high.astype(np.float32)).astype(jnp.bfloat16)


def dot(a, b):
    return jnp.dot(a, b, preferred_element_type=F32)


def dot_nt(a, b):
    return lax.dot_general(a, b, (((1,), (1,)), ((), ())), preferred_element_type=F32)


def wide(x, w_high, w_low):
    rows = x.shape[0]
    high, low = halves(x)
    both = dot(jnp.concatenate([high, low], axis=0), w_high)
    return both[:rows] + both[rows:] + dot(high, w_low)


def kernel(
    replicas, shards, unroll, total,
    grad_ref, mom_ref, idx_ref, fwd_ref, inv_ref, rows_ref, rows3_ref,
    newm_ref, upd_ref,
    by_span, picks, values, factor, ids, all_ids, shipped, all_values,
    span_a, span_b, span_v, dense, e_out, e_in,
    id_sem, value_sem, e_send, e_recv,
):
    me = lax.axis_index("dp")
    part = lax.axis_index("tensor")
    barrier = pltpu.get_barrier_semaphore()

    def greet_dp(k, c):
        pl.semaphore_signal(barrier, inc=1, device_id={"dp": lax.rem(me + k, replicas)}, device_id_type=MESH)
        return c

    def greet_tp(k, c):
        pl.semaphore_signal(barrier, inc=1, device_id={"tensor": lax.rem(part + k, shards)}, device_id_type=MESH)
        return c

    lax.fori_loop(1, replicas, greet_dp, 0)
    lax.fori_loop(1, shards, greet_tp, 0)

    topk, spans = idx_ref.shape
    fold = LANES // topk
    width = fold * BLOCK
    groups = spans // fold

    by_span[...] = idx_ref[...].T
    chosen = jnp.concatenate(
        [by_span[pl.ds(s, groups, stride=fold), :] for s in range(fold)], axis=1
    )
    ids[...] = chosen.astype(jnp.int16)
    picks[0] = (chosen // BLOCK).astype(F32)
    slot = lax.broadcasted_iota(jnp.int32, chosen.shape, 1) // topk
    picks[1] = (chosen % BLOCK + BLOCK * slot).astype(F32)

    zero = jnp.zeros((), BF16)
    one = jnp.ones((), BF16)
    tall = lax.broadcasted_iota(jnp.int32, (width, LANES), 0).astype(F32).astype(BF16)
    short = lax.broadcasted_iota(jnp.int32, (BLOCK, LANES), 0).astype(F32).astype(BF16)

    def hot(levels, plane, g):
        return jnp.where(levels == picks[plane, pl.ds(g, 1), :].astype(BF16), one, zero)

    def columns(g, size):
        return pl.ds(pl.multiple_of(g * size, size), size)

    def renew(g):
        cols = columns(g, width)
        return DECAY * mom_ref[:, cols].astype(F32) + grad_ref[:, cols].astype(F32)

    def encode(step, c):
        batch = [step * unroll + u for u in range(unroll)]
        half_spec = wide(jnp.concatenate([renew(g) for g in batch], axis=0), fwd_ref[0], fwd_ref[1])
        high, low = halves(half_spec)
        found = []
        for u, g in enumerate(batch):
            rows = slice(u * BLOCK, (u + 1) * BLOCK)
            both = dot(jnp.concatenate([high[rows], low[rows]], axis=0), hot(tall, 1, g))
            row_hot = hot(short, 0, g)
            waves = dot(rows_ref[...], jnp.concatenate([row_hot, row_hot], axis=0))
            value = jnp.sum((both[:BLOCK] + both[BLOCK:]) * waves, axis=0, keepdims=True)
            found.append((value, halves(waves * value)))
        for g, (value, pair) in zip(batch, found):
            values[pl.ds(g, 1), :] = value
            factor[:, columns(g, 2 * LANES)] = jnp.concatenate(pair, axis=1)
        return c

    def restore(step, c):
        batch = [step * unroll + u for u in range(unroll)]
        spread = []
        for g in batch:
            col_hot = hot(tall, 1, g)
            spread.append(dot_nt(factor[:, columns(g, 2 * LANES)], jnp.concatenate([col_hot, col_hot], axis=1)))
        restored = wide(jnp.concatenate(spread, axis=0), inv_ref[0], inv_ref[1])
        for u, g in enumerate(batch):
            newm_ref[:, columns(g, width)] = (renew(g) - restored[u * BLOCK:(u + 1) * BLOCK]).astype(BF16)
        return c

    def copy_dp(src, dst, sems, k, slot):
        return pltpu.make_async_remote_copy(
            src_ref=src, dst_ref=dst.at[slot],
            send_sem=sems.at[0, k], recv_sem=sems.at[1, k],
            device_id={"dp": lax.rem(me + k, replicas)}, device_id_type=MESH,
        )

    def to_all(src, dst, sems):
        def start(k, c):
            copy_dp(src, dst, sems, k, me).start()
            return c
        lax.fori_loop(1, replicas, start, 0)
        dst[me] = src[...]

    def from_all(src, dst, sems):
        def finish(k, c):
            copy_dp(src, dst, sems, k, lax.rem(me - k + replicas, replicas)).wait_recv()
            return c
        lax.fori_loop(1, replicas, finish, 0)

    def sent_all(src, dst, sems):
        def finish(k, c):
            copy_dp(src, dst, sems, k, me).wait_send()
            return c
        lax.fori_loop(1, replicas, finish, 0)

    steps = groups // unroll
    lax.fori_loop(0, steps // 2, encode, 0)
    pl.semaphore_wait(barrier, replicas - 1 + shards - 1)
    to_all(ids, all_ids, id_sem)
    lax.fori_loop(steps // 2, steps, encode, 0)
    shipped[...] = values[...].astype(BF16)
    to_all(shipped, all_values, value_sem)
    lax.fori_loop(0, steps, restore, 0)
    from_all(ids, all_ids, id_sem)
    from_all(shipped, all_values, value_sem)

    for s in range(fold):
        lines = slice(s * groups, (s + 1) * groups)
        lanes = slice(s * topk, (s + 1) * topk)
        span_v[lines, :] = jnp.concatenate([all_values[r].astype(F32)[:, lanes] for r in range(replicas)], axis=1)
        named = jnp.concatenate([all_ids[r].astype(jnp.int32)[:, lanes] for r in range(replicas)], axis=1)
        span_a[lines, :] = (named // BLOCK).astype(F32)
        span_b[lines, :] = (named % BLOCK).astype(F32)

    depth = replicas * topk
    level = lax.broadcasted_iota(jnp.int32, (BLOCK, depth), 0).astype(F32).astype(BF16)

    def densify(step, energy):
        tiles = []
        for s in range(fold):
            lines = pl.ds(pl.multiple_of(s * groups + step * 8, 8), 8)
            tiles.append([ref[lines, :] for ref in (span_a, span_b, span_v)])
        for u in range(8):
            blocks = []
            for s in range(fold):
                a, b, v = (tile[u:u + 1].astype(BF16) for tile in tiles[s])
                row_hot = jnp.where(level == a, v, zero)
                col_hot = jnp.where(level == b, one, zero)
                blocks.append(dot_nt(row_hot, col_hot))
            combined = jnp.concatenate(blocks, axis=1)
            dense[:, columns(step * 8 + u, width)] = combined
            energy = energy + jnp.sum((combined * combined).reshape(BLOCK // 8, 8, width), axis=0)
        return energy

    energy = lax.fori_loop(0, groups // 8, densify, jnp.zeros((8, width), F32))
    energy = sum(energy[:, n * LANES:(n + 1) * LANES] for n in range(width // LANES))
    e_out[...] = energy
    e_in[part] = energy

    def copy_tp(k, slot):
        return pltpu.make_async_remote_copy(
            src_ref=e_out, dst_ref=e_in.at[slot],
            send_sem=e_send.at[k], recv_sem=e_recv.at[k],
            device_id={"tensor": lax.rem(part + k, shards)}, device_id_type=MESH,
        )

    def start_tp(k, c):
        copy_tp(k, part).start()
        return c

    lax.fori_loop(1, shards, start_tp, 0)

    def decode(step, c):
        batch = [columns(step * unroll + u, width) for u in range(unroll)]
        across = wide(jnp.concatenate([dense[:, cols] for cols in batch], axis=0), inv_ref[0], inv_ref[1])
        high, low = halves(across)
        done = []
        for u in range(unroll):
            rows = slice(u * BLOCK, (u + 1) * BLOCK)
            done.append(dot(rows3_ref[...], jnp.concatenate([high[rows], high[rows], low[rows]], axis=0)))
        for cols, block in zip(batch, done):
            dense[:, cols] = block
        return c

    lax.fori_loop(0, groups // unroll, decode, 0)

    def finish_tp(k, c):
        copy_tp(k, lax.rem(part - k + shards, shards)).wait()
        return c

    lax.fori_loop(1, shards, finish_tp, 0)
    mean = jnp.sum(e_in[...]) / total
    scale = lax.rsqrt(jnp.full((1, width), mean + EPSILON, F32))

    def finish(step, c):
        for u in range(unroll):
            cols = columns(step * unroll + u, width)
            upd_ref[:, cols] = (dense[:, cols] * scale).astype(BF16)
        return c

    lax.fori_loop(0, groups // unroll, finish, 0)
    sent_all(ids, all_ids, id_sem)
    sent_all(shipped, all_values, value_sem)


def local(gradient, momentum, indices, replicas, shards):
    height, cols = gradient.shape[1:]
    topk = indices.shape[-1]
    fold = LANES // topk
    spans = cols // BLOCK
    groups = spans // fold
    assert height == BLOCK and groups * fold == spans
    basis = dct_basis(BLOCK)
    eye = np.eye(fold, dtype=np.float32)
    fwd = jnp.asarray(np.stack(np_halves(np.kron(eye, basis.T))))
    inv = jnp.asarray(np.stack(np_halves(np.kron(eye, basis))))
    high, low = np_halves(basis.T)
    rows = jnp.asarray(np.concatenate([high, low], axis=1))
    rows3 = jnp.asarray(np.concatenate([high, low, high], axis=1))
    depth = max(replicas * topk, LANES)
    vmem = pl.BlockSpec(memory_space=pltpu.VMEM)
    newm, update = pl.pallas_call(
        functools.partial(kernel, replicas, shards, 8, float(height * cols * shards)),
        out_shape=(
            jax.ShapeDtypeStruct((height, cols), BF16),
            jax.ShapeDtypeStruct((height, cols), BF16),
        ),
        in_specs=[vmem] * 7,
        out_specs=(vmem, vmem),
        scratch_shapes=[
            pltpu.VMEM((spans, topk), jnp.int32),
            pltpu.VMEM((2, groups, LANES), F32),
            pltpu.VMEM((groups, LANES), F32),
            pltpu.VMEM((height, groups * 2 * LANES), BF16),
            pltpu.VMEM((groups, LANES), jnp.int16),
            pltpu.VMEM((replicas, groups, LANES), jnp.int16),
            pltpu.VMEM((groups, LANES), BF16),
            pltpu.VMEM((replicas, groups, LANES), BF16),
            pltpu.VMEM((spans, depth), F32),
            pltpu.VMEM((spans, depth), F32),
            pltpu.VMEM((spans, depth), F32),
            pltpu.VMEM((height, cols), F32),
            pltpu.VMEM((8, LANES), F32),
            pltpu.VMEM((shards, 8, LANES), F32),
            pltpu.SemaphoreType.DMA((2, replicas)),
            pltpu.SemaphoreType.DMA((2, replicas)),
            pltpu.SemaphoreType.DMA((shards,)),
            pltpu.SemaphoreType.DMA((shards,)),
        ],
        compiler_params=pltpu.CompilerParams(collective_id=0, has_side_effects=True),
        name="demo_step",
    )(gradient[0], momentum[0], indices.reshape(spans, topk).T, fwd, inv, rows, rows3)
    return newm[None], update


def solution(mesh):
    in_specs = (P("dp", "tensor", None), P("dp", "tensor", None), P("dp", "tensor", None, None))
    out_specs = (P("dp", "tensor", None), P("tensor", None))
    body = functools.partial(local, replicas=mesh.shape["dp"], shards=mesh.shape["tensor"])
    return jax.shard_map(body, mesh=mesh, in_specs=in_specs, out_specs=out_specs, check_vma=False)
```

time: 50.4 us -> 28.3 us (0.56)
  Pallas kernels: 44.7 us -> 24.1 us
  local copies, waits for them, and re-layouts: 4.77 us -> 3.32 us
    pallas_call x1, Pallas kernels: 44.7 us -> 24.1 us  [local(): pl.pallas_call(functools.partial(kernel, replicas, shards, 8, float(heigh...]
    unnamed x5 -> x4, local copies, waits for them, and re-layouts: 4.77 us -> 3.32 us
where the time goes in v2:
time: 28.3 us; the launch traced here: 28.1 us
  Pallas kernels  24.1 us (85%)
  local copies, waits for them, and re-layouts  3.32 us (12%)
  between operations  0.65 us (2%)
    pallas_call x1, Pallas kernels, local(): pl.pallas_call(functools.partial(kernel, replicas, shards, 8, float(heigh...  24.1 us
    unnamed x4, local copies, waits for them, and re-layouts  3.32 us

profile of v2, /device:TPU:0, one launch (start us, length us, event | category | flops | bytes accessed | tf_op | source)
XLA Modules:
  0.0 28.1 jit_solution(4556157818871999355)
XLA Ops:
  0.6 24.1 %demo_step.1 = (bf16[64,8192]{1,0:T(8,128)(2,1)}, bf16[64,8192]{1,0:T(8,128)(2,1)}) custom-call(bf16[64,8192]{1,0:T(8,128)(2,1)} %bitcast.7, bf16[64,8192]{1,0:T(8,128)(2,1)} %bitcast.8, s32[32,128]{1,0:T(8,128)} %bitcast.9, bf16[2,256,256]{2,1,0:T(8,128)(2,1)} %constant.8.clone.fwd_ref, bf16[2,256,256]{2,1,0:T(8,128)(2,1)} %constant.9.clone.inv_ref, ...), custom_call_target="tpu_custom_call" | custom-call | tf_op jit(solution)/shard_map/demo_step/pallas_call | solution.py:265
  24.8 0.0 copy-start
  24.8 2.4 %copy.11 = bf16[1,64,8192]{2,1,0:T(8,128)(2,1)} copy(bf16[1,64,8192]{2,1,0:T(8,128)(2,1)} %bitcast.6) | data formatting | bytes 2097152
  27.1 0.0 copy-done
  27.1 1.0 %copy.12 = bf16[64,8192]{1,0:T(8,128)(2,1)} copy(bf16[64,8192]{1,0:T(8,128)(2,1)S(1)} %copy-done) | data formatting | bytes 2097152
Async XLA Ops:
  24.8 2.4 %copy-start = (bf16[64,8192]{1,0:T(8,128)(2,1)S(1)}, bf16[64,8192]{1,0:T(8,128)(2,1)}, u32[]{:S(2)}) copy-start(bf16[64,8192]{1,0:T(8,128)(2,1)} %get-tuple-element.9) | copy-start | bytes 3145732
